TPU v7x, 32 devices: a whole 2x2x4 slice. The times are simulated.
32 devices in a mesh: sub: 4 (over y, x), elem: 8 (over z, core).
Axes of the slice: x: 2, y: 2, z: 4, core: 2. Of those that a mesh axis runs over, the one named last changes fastest.
Arguments:
- element_tiles: bfloat16 [256, 128, 128], P(('sub', 'elem')), parts along dimension 0, may hold values from -0.5 to 0.5
- element_blocks: int32 [256, 2], P(('sub', 'elem')), parts along dimension 0, may hold values from 0 to 31
- mode_shapes: bfloat16 [16384, 1024], P(('sub', 'elem')), parts along dimension 0, may hold values from -0.5 to 0.5
- trial_modes: bfloat16 [4096, 128], P('sub'), parts along dimension 0, may hold values from -0.1875 to 0.1875
Outputs:
- reduced_stiffness: float32 [4096, 1024], P(('sub', 'elem')), parts along dimension 0
- interface_forces: float32 [4096, 128], P(('sub', 'elem')), parts along dimension 0
There are 4 independent parts, one for each index of `sub`. A program takes and returns all parts, laid end to end along the dimension named above; each array names one. Nothing has to cross between parts.
Inputs may be any that keep to these rules, and one draw needn't show every extreme that they name: `element_blocks`: each row gives the row block and the column block of one element tile.
All inputs are finite; a program needn't handle non-finite values.
Results may differ from a plain program's by a relative error of at most 0.0029.
Values may be sent and summed in bfloat16 or wider, within the bound.
No kernel may reach another device: no remote copies, remote signals or barrier semaphores. Data moves between devices by JAX's collectives and lax.ppermute only.
A program may use at most 64 MiB of HBM per device.

v0:
```python
import jax
import jax.numpy as jnp
from jax import lax
from jax.sharding import PartitionSpec as P


def project(row_side, stiff_modes):
    return lax.dot_general(
        row_side, stiff_modes, (((0,), (0,)), ((), ())), preferred_element_type=jnp.float32
    )


def body(element_tiles, element_blocks, mode_shapes, trial_modes):
    gathered = lax.all_gather(mode_shapes, "elem", axis=0, tiled=True)
    block_width = element_tiles.shape[1]
    mode_count = gathered.shape[1]
    blocks = gathered.reshape(-1, block_width, mode_count)
    row_side = jnp.take(blocks, element_blocks[:, 0], axis=0).reshape(-1, mode_count)
    col_side = jnp.take(blocks, element_blocks[:, 1], axis=0)
    stiff_modes = jnp.einsum(
        "eij,ejm->eim", element_tiles, col_side, preferred_element_type=jnp.float32
    )
    stiff_modes = stiff_modes.astype(jnp.bfloat16).reshape(-1, mode_count)
    reduced = lax.psum_scatter(
        project(row_side, stiff_modes), "elem", scatter_dimension=0, tiled=True
    )
    forces = jnp.dot(reduced, trial_modes.astype(jnp.float32), precision=lax.Precision.HIGHEST)
    return (reduced, forces)


def solution(mesh):
    in_specs = (
        P(("sub", "elem"), None, None),
        P(("sub", "elem"), None),
        P(("sub", "elem"), None),
        P("sub", None),
    )
    out_specs = (P(("sub", "elem"), None), P(("sub", "elem"), None))
    return jax.shard_map(body, mesh=mesh, in_specs=in_specs, out_specs=out_specs, check_vma=False)
```

profile of v0, /device:TPU:0, one launch (start us, length us, event | category | flops | bytes accessed | tf_op | source)
XLA Modules:
  0.0 167.9 jit_solution(1914084486754698559)
XLA Ops:
  7.2 0.0 copy-start
  7.2 0.0 all-gather.2.cloned.1.call-start
  7.2 0.7 all-gather.2.cloned.1.call-update
  7.9 0.0 reduce-scatter.2.cloned.1.call-start
  8.0 0.8 compare_and_fusion
  8.7 85.6 %all-gather.2.cloned.1.call-done = bf16[4096,1024]{1,0:T(8,128)(2,1)} async-done(((bf16[512,1024]{1,0:T(8,128)(2,1)}), bf16[4096,1024]{1,0:T(8,128)(2,1)}) %all-gather.2.cloned.1.call-update) | async-done | bytes 8388624 | tf_op jit(solution)/shard_map/all_gather | solution.py:14
  94.4 4.1 %gather_fusion.1 = bf16[8,128,1024]{2,1,0:T(8,128)(2,1)S(1)} fusion(bf16[32,128,1024]{2,1,0:T(8,128)(2,1)} %bitcast.15, s32[1024]{0:T(1024)S(1)} %get-tuple-element.9), kind=kCustom, calls=%fused_computation.1.clone | custom fusion | bytes 4194336 | tf_op jit(solution)/shard_map/jit(_take)/gather | solution.py:19
  98.4 5.4 %gather_fusion = bf16[8,128,1024]{2,1,0:T(8,128)(2,1)} fusion(bf16[32,128,1024]{2,1,0:T(8,128)(2,1)} %bitcast.16, s32[1024]{0:T(1024)S(1)} %get-tuple-element.10), kind=kCustom, calls=%fused_computation.clone | custom fusion | bytes 4194336 | tf_op jit(solution)/shard_map/jit(_take)/gather | solution.py:18
  103.9 0.0 copy-done
  103.9 6.5 %convolution_bitcast_fusion = f32[1024,1024]{1,0:T(8,128)} fusion(bf16[8,128,1024]{2,1,0:T(8,128)(2,1)} %gather_fusion, bf16[8,128,128]{2,1,0:T(8,128)(2,1)S(1)} %copy-done, bf16[8,128,1024]{2,1,0:T(8,128)(2,1)S(1)} %gather_fusion.1, pred[8]{0:T(512)(128)(4,1)S(1)} %get-tuple-element.5, pred[8]{0:T(512)(128)(4,1)S(1)} %get-tuple-element.7), kind=kOutput, calls=%fused_computation.2 | convolution fusion | flops 2419064832 | bytes 8650768 | tf_op jit(solution)/shard_map/dot_general | solution.py:8
  110.4 0.0 copy-start.1
  110.4 0.0 reduce-scatter.2.cloned.1.call-update
  110.4 48.6 %reduce-scatter.2.cloned.1.call-done = f32[128,1024]{1,0:T(8,128)} async-done(((f32[1024,1024]{1,0:T(8,128)}), f32[128,1024]{1,0:T(8,128)}) %reduce-scatter.2.cloned.1.call-update) | async-done | bytes 524304 | tf_op jit(solution)/shard_map/reduce_scatter | solution.py:24
  159.0 0.0 copy-done.1
  159.0 2.0 %fusion.15 = f32[128,128]{1,0:T(8,128)} fusion(f32[128,1024]{1,0:T(8,128)} %reduce-scatter.2.cloned.1.call-done, bf16[1024,128]{1,0:T(8,128)(2,1)S(1)} %copy-done.1), kind=kOutput, calls=%fused_computation.18 | convolution fusion | flops 201326592 | bytes 851968 | tf_op jit(solution)/shard_map/dot_general | solution.py:27
  (1 shorter events, 0.0 us)
Async XLA Ops:
  7.2 96.7 %copy-start = (bf16[8,128,128]{2,1,0:T(8,128)(2,1)S(1)}, bf16[8,128,128]{2,1,0:T(8,128)(2,1)}, u32[]{:S(2)}) copy-start(bf16[8,128,128]{2,1,0:T(8,128)(2,1)} %param.6) | copy-start | bytes 786436
  7.2 87.2 %all-gather.2.cloned.1.call-start = ((), (), s32[]{:S(2)}) async-start(), calls=%async_computation.1 | async-start | bytes 9437184 | tf_op jit(solution)/shard_map/all_gather | solution.py:14
  7.9 151.1 %reduce-scatter.2.cloned.1.call-start = ((), (), s32[]{:S(2)}) async-start(), calls=%async_computation.2 | async-start | bytes 4718592 | tf_op jit(solution)/shard_map/reduce_scatter | solution.py:24
  110.4 48.6 %copy-start.1 = (bf16[1024,128]{1,0:T(8,128)(2,1)S(1)}, bf16[1024,128]{1,0:T(8,128)(2,1)}, u32[]{:S(2)}) copy-start(bf16[1024,128]{1,0:T(8,128)(2,1)} %param.9) | copy-start | bytes 786436
Sparse Core Ops, SparseCore 0:
  9.6 84.7 all-gather.1
  110.5 48.4 reduce-scatter.1
where the time goes:
time: 168 us
  waiting for transfers between devices  135 us (80%)
  between operations  14.1 us (8%)
  local copies, waits for them, and re-layouts  9.49 us (6%)
  matrix products  8.56 us (5%)
    all_gather x1, waiting for transfers between devices, body(): gathered = lax.all_gather(mode_shapes, 'elem', axis=0, tiled=True)  85.6 us
    reduce_scatter x1, waiting for transfers between devices, body(): lax.psum_scatter(project(row_side, stiff_modes), 'elem', scatter_dimensio...  48.6 us
    dot_general x1, matrix products, project(): lax.dot_general(row_side, stiff_modes, (((0,), (0,)), ((), ())), preferre...  6.52 us
    gather x1, local copies, waits for them, and re-layouts, body(): jnp.take(blocks, element_blocks[:, 0], axis=0).reshape(-1, mode_count)  5.42 us
    gather x1, local copies, waits for them, and re-layouts, body(): col_side = jnp.take(blocks, element_blocks[:, 1], axis=0)  4.06 us
  transfers between devices with their start and end apart: 2, of which 2 were waited for; matrix products, arithmetic and copies ran while one was open for 0% of the time, Pallas kernels for 0%

commit v1 on v0

v1 whole, which is shorter than its diff:
```python
import functools

import jax
import jax.numpy as jnp
from jax import lax
from jax.experimental import pallas as pl
from jax.experimental.pallas import tpu as pltpu
from jax.sharding import PartitionSpec as P


AXES = ("sub", "elem")
LANES, BELOW = 128, 8
SPARE = 3 << 20
SMEM = pl.BlockSpec(memory_space=pltpu.SMEM)
VMEM = pl.BlockSpec(memory_space=pltpu.VMEM)
ANY = pl.BlockSpec(memory_space=pl.ANY)
HBM = pl.BlockSpec(memory_space=pltpu.HBM)


class Plan:
    def __init__(self, mesh):
        self.parts, self.places = mesh.shape["sub"], mesh.shape["elem"]
        self.chips = self.places // 2
        self.root = self.chips // 2 - 1
        self.beyond = self.root + 1
        self.paired = self.parts % 4 == 0
        self.flips = (1, 2) if self.paired else ()

    def kind(self, part):
        return (part ^ (part >> 1)) & 1 if self.paired else part * 0

    def device(self, part, step, core):
        chip = self.chips - 1 - step if self.kind(part) else step
        return part * self.places + chip * 2 + core

    def beside(self, part, step, core, flip):
        return self.device(part, step, core) + ((part ^ flip) - part) * self.places

    def pairs(self, route):
        return [route(part, core) for part in range(self.parts) for core in range(2)]

    def to_root(self, step):
        return self.pairs(lambda p, c: (self.device(p, step, c), self.device(p, self.root, c)))

    def aside(self, step, flip):
        return self.pairs(lambda p, c: (self.device(p, step, c), self.beside(p, step, c, flip)))

    def aside_to_root(self, step, flip):
        return self.pairs(lambda p, c: (self.beside(p, step, c, flip), self.device(p, self.root, c)))

    def swap(self):
        return self.pairs(lambda p, c: (self.device(p, self.root, c), self.device(p, self.root, 1 - c)))

    def from_root(self, step, cross):
        return self.pairs(lambda p, c: (self.device(p, self.root, c), self.device(p, step, c ^ cross)))


def pack_kernel(cuts, p_ref, t_ref, b_ref, all_ref, *rest):
    parts, low_ref, sems = rest[:-2], rest[-2], rest[-1]
    depth, modes = p_ref.shape
    local, width, _ = t_ref.shape
    per = depth // width
    copies = [pltpu.make_async_copy(p_ref, all_ref.at[pl.ds(0, depth), pl.ds(0, modes)], sems.at[local])]
    for t in range(local):
        row, column = t % per * width, modes + t // per * width
        copies.append(
            pltpu.make_async_copy(t_ref.at[t], all_ref.at[pl.ds(row, width), pl.ds(column, width)], sems.at[t])
        )
    for copy in copies:
        copy.start()
    low_ref[...] = jnp.zeros_like(low_ref)
    low_ref[: b_ref.shape[0], :local] = b_ref[...]
    all_ref[depth:, :] = jnp.zeros((BELOW, all_ref.shape[1]), all_ref.dtype)
    all_ref[depth:, :LANES] = low_ref[...].astype(jnp.float32).astype(all_ref.dtype)
    for copy in copies:
        copy.wait()
    for i, part in enumerate(parts):
        low, high = cuts[i], cuts[i + 1]
        part[: high - low, :] = all_ref[low:high, :]
        if part.shape[0] > high - low:
            part[high - low :, :] = all_ref[depth:, :]


def join_kernel(cuts, *refs):
    parts, all_ref = refs[:-1], refs[-1]
    for part, low, high in zip(parts, cuts[:-1], cuts[1:]):
        all_ref[low:high, :] = part[: high - low, :]
        if part.shape[0] > high - low:
            all_ref[cuts[-1] :, :] = part[high - low :, :]


def root_kernel(plan, spans, width, modes, elems, where_ref, *refs):
    chips, n, half, below = plan.chips, len(spans), modes // 2, BELOW
    p_in, outs = refs[:n], refs[n : n + 2 * chips]
    p_all, t_all, low_idx, vec_idx, idx, q_sum, q_low, k_acc, sems = refs[n + 2 * chips :]
    kind, core = where_ref[0], where_ref[1]
    depth, local = p_all.shape[0] // plan.places, elems // plan.places
    per = depth // width
    mine = pl.ds(pl.multiple_of(core * half, half), half)
    rest = pl.ds(pl.multiple_of((1 - core) * half, half), half)

    first, second, numbers = [], [], []
    for i, (row, rows) in enumerate(spans):
        src, to = pl.ds(0, rows), pl.ds(row, rows)
        if p_in[i].shape[0] > rows:
            slot = row // depth
            numbers.append(
                pltpu.make_async_copy(
                    p_in[i].at[pl.ds(rows, below), pl.ds(0, LANES)],
                    low_idx.at[pl.ds(slot * below, below), :],
                    sems.at[3 * n + i],
                )
            )
        first.append(
            pltpu.make_async_copy(p_in[i].at[src, pl.ds(modes, t_all.shape[1])], t_all.at[to, :], sems.at[n + i])
        )
        first.append(pltpu.make_async_copy(p_in[i].at[src, mine], p_all.at[to, mine], sems.at[i]))
        second.append(pltpu.make_async_copy(p_in[i].at[src, rest], p_all.at[to, rest], sems.at[2 * n + i]))
    for copy in numbers + first + second:
        copy.start()
    for copy in numbers:
        copy.wait()
    vec_idx[...] = low_idx[...].astype(jnp.float32).astype(jnp.int32)
    to_smem = pltpu.make_async_copy(vec_idx, idx, sems.at[4 * n])
    to_smem.start()
    q_sum[...] = jnp.zeros_like(q_sum)
    to_smem.wait()
    for copy in first:
        copy.wait()

    def row_of(block):
        place, b = block // per, block % per
        chip, other = place // 2, (place % 2) ^ core
        step = jnp.where(kind == 1, chips - 1 - chip, chip)
        return pl.ds(pl.multiple_of(((step * 2 + other) * per + b) * width, width), width)

    def element(e, carry):
        slot, t = e // local, e % local
        tile = t_all[
            pl.ds(pl.multiple_of(slot * depth + t % per * width, width), width),
            pl.ds(pl.multiple_of(t // per * width, width), width),
        ]
        r, c = idx[slot * below, t], idx[slot * below + 1, t]
        stiff = jnp.dot(tile, p_all[row_of(c), mine], preferred_element_type=jnp.float32).astype(jnp.bfloat16)
        q_sum[row_of(r), :] += stiff.astype(jnp.float32)
        return carry

    lax.fori_loop(0, elems, element, 0, unroll=8)
    for copy in second:
        copy.wait()
    chunk = p_all.shape[0] // 4
    for i in range(4):
        rows = pl.ds(i * chunk, chunk)
        q_low[rows, :] = q_sum[rows, :].astype(jnp.bfloat16)
        part = lax.dot_general(
            p_all[rows, :], q_low[rows, :], (((0,), (0,)), ((), ())), preferred_element_type=jnp.float32
        )
        if i == 0:
            k_acc[...] = part
        else:
            k_acc[...] += part
    strip = modes // plan.places
    for step in range(chips):
        chip = jnp.where(kind == 1, chips - 1 - step, step)
        for cross in range(2):
            row = pl.multiple_of((chip * 2 + (core ^ cross)) * strip, strip)
            outs[2 * step + cross][...] = k_acc[pl.ds(row, strip), :].astype(jnp.bfloat16)


def final_kernel(n, where_ref, trial_ref, *refs):
    same, cross = refs[:n], refs[n : 2 * n]
    k_ref, f_ref, rows = refs[2 * n :]
    core, step = where_ref[1], where_ref[2]
    half = same[0].shape[1]
    mine = pl.ds(pl.multiple_of(core * half, half), half)
    other = pl.ds(pl.multiple_of((1 - core) * half, half), half)
    for i in range(n):

        @pl.when(step == i)
        def _():
            rows[:, mine] = same[i][...]
            rows[:, other] = cross[i][...]

    k = rows[...]
    k_ref[...] = k.astype(jnp.float32)
    f_ref[...] = jnp.dot(k, trial_ref[...], preferred_element_type=jnp.float32)


def body(plan, element_tiles, element_blocks, mode_shapes, trial_modes):
    part, place = lax.axis_index("sub"), lax.axis_index("elem")
    kind, core, chip = plan.kind(part), place % 2, place // 2
    step = jnp.where(kind == 1, plan.chips - 1 - chip, chip)
    where = jnp.stack([kind, core, step]).astype(jnp.int32)
    local, width, _ = element_tiles.shape
    depth, modes = mode_shapes.shape
    root, chips, beyond = plan.root, plan.chips, plan.beyond
    per = depth // width
    wide = modes + local // per * width
    total, elems = depth * plan.places, local * plan.places
    strip, half = modes // plan.places, modes // 2

    def send(x, pairs):
        return lax.ppermute(x, AXES, pairs)

    def kernel(fn, out, ins, scratch, limit, flops=0):
        return pl.pallas_call(
            fn,
            out_shape=out,
            in_specs=ins,
            out_specs=[VMEM] * len(out),
            scratch_shapes=scratch,
            compiler_params=pltpu.CompilerParams(vmem_limit_bytes=limit + SPARE),
            cost_estimate=pl.CostEstimate(flops=flops, bytes_accessed=0, transcendentals=0),
        )

    def array(shape, dtype=jnp.bfloat16):
        return jax.ShapeDtypeStruct(shape, dtype)

    cuts = (0, depth // 4, depth // 4 + (depth - depth // 4) // 2, depth) if plan.paired else (0, depth)
    heights = [high - low for low, high in zip(cuts[:-1], cuts[1:])]
    carrier = 1 if plan.paired else 0
    shard, *parts = kernel(
        functools.partial(pack_kernel, cuts),
        [array((depth + BELOW, wide))] + [array((n + BELOW * (i == carrier), wide)) for i, n in enumerate(heights)],
        [HBM, HBM, VMEM],
        [pltpu.VMEM((BELOW, LANES), jnp.int32), pltpu.SemaphoreType.DMA((local + 1,))],
        4 * depth * wide,
    )(mode_shapes, element_tiles, element_blocks.T)

    got = {root: shard}
    sides = [send(x, plan.aside(beyond, f)) for x, f in zip(parts[1:], plan.flips)]
    for s in range(chips - 1, -1, -1):
        if s not in (root, beyond):
            got[s] = send(shard, plan.to_root(s))
    cut = [send(parts[0], plan.to_root(beyond))]
    cut += [send(x, plan.aside_to_root(beyond, f)) for x, f in zip(sides, plan.flips)]
    [got[beyond]] = kernel(
        functools.partial(join_kernel, cuts), [array((depth + BELOW, wide))], [VMEM] * len(cut), [], 4 * depth * wide
    )(*cut)

    p_in, spans = [], []
    for s in range(chips):
        p_in += [got[s], send(got[s], plan.swap())]
        spans += [(2 * s * depth, depth), ((2 * s + 1) * depth, depth)]

    pieces = kernel(
        functools.partial(root_kernel, plan, spans, width, modes, elems),
        [array((strip, half))] * plan.places,
        [SMEM] + [ANY] * len(p_in),
        [
            pltpu.VMEM((total, modes), jnp.bfloat16),
            pltpu.VMEM((total, wide - modes), jnp.bfloat16),
            pltpu.VMEM((plan.places * BELOW, LANES), jnp.bfloat16),
            pltpu.VMEM((plan.places * BELOW, LANES), jnp.int32),
            pltpu.SMEM((plan.places * BELOW, LANES), jnp.int32),
            pltpu.VMEM((total, half), jnp.float32),
            pltpu.VMEM((total, half), jnp.bfloat16),
            pltpu.VMEM((modes, half), jnp.float32),
            pltpu.SemaphoreType.DMA((4 * len(p_in) + 1,)),
        ],
        total * (wide + 3 * half) * 2 + 8 * modes * half,
        2 * elems * width * width * half + 2 * total * modes * half,
    )(where, *p_in)
    same = [pieces[2 * s] if s == root else send(pieces[2 * s], plan.from_root(s, 0)) for s in range(chips)]
    cross = [send(pieces[2 * s + 1], plan.from_root(s, 1)) for s in range(chips)]
    return kernel(
        functools.partial(final_kernel, chips),
        [array((strip, modes), jnp.float32), array((strip, trial_modes.shape[1]), jnp.float32)],
        [SMEM] + [VMEM] * (2 * chips + 1),
        [pltpu.VMEM((strip, modes), jnp.bfloat16)],
        4 << 20,
    )(where, trial_modes, *same, *cross)


def solution(mesh):
    plan = Plan(mesh)
    in_specs = (
        P(AXES, None, None),
        P(AXES, None),
        P(AXES, None),
        P("sub", None),
    )
    out_specs = (P(AXES, None), P(AXES, None))

    def step(*args):
        return body(plan, *args)

    return jax.shard_map(step, mesh=mesh, in_specs=in_specs, out_specs=out_specs, check_vma=False)
```

time: 168 us -> 90.4 us (0.54)
  the two profiles are of different devices: /device:TPU:0 before, /device:TPU:3 now
where the time goes in v1:
time: 90.4 us; the launch traced here: 89.9 us
  waiting for transfers between devices  47.9 us (53%)
  starting transfers between devices  23.3 us (26%)
  Pallas kernels  14.9 us (16%)
  local copies, waits for them, and re-layouts  2.85 us (3%)
    ppermute x18, waiting for transfers between devices, send(): return lax.ppermute(x, AXES, pairs)  47.9 us
    ppermute x18, starting transfers between devices, send(): return lax.ppermute(x, AXES, pairs)  23.3 us
    pallas_call x1, Pallas kernels, body(): kernel(functools.partial(root_kernel, plan, spans, width, modes, elems),...  13 us
    unnamed x8, local copies, waits for them, and re-layouts  2.85 us
  transfers between devices with their start and end apart: 18, of which 3 were waited for; matrix products, arithmetic and copies ran while one was open for 0% of the time, Pallas kernels for 0%

profile of v1, /device:TPU:3, one launch (start us, length us, event | category | flops | bytes accessed | tf_op | source)
XLA Modules:
  0.0 89.9 jit_solution(12041074835246425966)
XLA Ops:
  0.6 0.0 copy-start
  0.6 1.2 %copy-done = bf16[512,1024]{1,0:T(8,128)(2,1)S(1)} copy-done((bf16[512,1024]{1,0:T(8,128)(2,1)S(1)}, bf16[512,1024]{1,0:T(8,128)(2,1)}, u32[]{:S(2)}) %copy-start) | copy-done | bytes 1048600
  1.9 0.0 copy-start.2
  1.9 0.9 %copy-done.2 = bf16[8,128,128]{2,1,0:T(8,128)(2,1)S(1)} copy-done((bf16[8,128,128]{2,1,0:T(8,128)(2,1)S(1)}, bf16[8,128,128]{2,1,0:T(8,128)(2,1)}, u32[]{:S(2)}) %copy-start.2) | copy-done | bytes 262168
  2.8 0.0 copy-start.3
  2.8 0.7 copy-done.3
  3.5 0.4 shard_map.59
  3.9 5.3 %collective-permute-start.9 = (bf16[520,1280]{1,0:T(8,128)(2,1)S(1)}, bf16[520,1280]{1,0:T(8,128)(2,1)}, u32[]{:S(2)}, u32[]{:S(2)}) collective-permute-start(bf16[520,1280]{1,0:T(8,128)(2,1)S(1)} %get-tuple-element.14.refs_2_), channel_id=1, source_target_pairs={{6,2},{7,3},{8,12},{9,13},{16,20},{17,21},{30,26},{31,27}} | collective-permute-start | bytes 3993608 | tf_op jit(solution)/shard_map/ppermute | solution.py:203
  9.2 1.7 %collective-permute-start = (bf16[520,1280]{1,0:T(8,128)(2,1)S(1)}, bf16[520,1280]{1,0:T(8,128)(2,1)}, u32[]{:S(2)}, u32[]{:S(2)}) collective-permute-start(bf16[520,1280]{1,0:T(8,128)(2,1)S(1)} %get-tuple-element.14.refs_2_), channel_id=1, source_target_pairs={{0,2},{1,3},{14,12},{15,13},{22,20},{23,21},{24,26},{25,27}} | collective-permute-start | bytes 3993608 | tf_op jit(solution)/shard_map/ppermute | solution.py:203
  10.9 0.7 collective-permute-start.4
  11.6 0.7 collective-permute-start.6
  12.3 0.0 collective-permute-done.4
  12.3 0.7 collective-permute-start.5
  13.0 0.0 collective-permute-done.6
  13.0 0.7 collective-permute-start.7
  13.7 0.7 collective-permute-start.3
  14.4 0.0 collective-permute-done.3.refs_0_
  14.4 1.8 %collective-permute-start.2 = (bf16[520,1280]{1,0:T(8,128)(2,1)S(1)}, bf16[520,1280]{1,0:T(8,128)(2,1)}, u32[]{:S(2)}, u32[]{:S(2)}) collective-permute-start(bf16[520,1280]{1,0:T(8,128)(2,1)S(1)} %get-tuple-element.14.refs_2_), channel_id=1, source_target_pairs={{2,3},{3,2},{12,13},{13,12},{20,21},{21,20},{26,27},{27,26}} | collective-permute-start | bytes 3993608 | tf_op jit(solution)/shard_map/ppermute | solution.py:203
  16.2 0.0 collective-permute-done.7.refs_2_
  16.2 0.0 collective-permute-done.5.refs_1_
  16.2 0.1 shard_map.60.refs_4_
  16.2 1.8 %collective-permute-start.8 = (bf16[520,1280]{1,0:T(8,128)(2,1)S(1)}, bf16[520,1280]{1,0:T(8,128)(2,1)}, u32[]{:S(2)}, u32[]{:S(2)}) collective-permute-start(bf16[520,1280]{1,0:T(8,128)(2,1)S(1)} %shard_map.60.refs_4_), channel_id=1, source_target_pairs={{2,3},{3,2},{12,13},{13,12},{20,21},{21,20},{26,27},{27,26}} | collective-permute-start | bytes 3993608 | tf_op jit(solution)/shard_map/ppermute | solution.py:203
  18.0 18.0 %collective-permute-done.9.refs_6_ = bf16[520,1280]{1,0:T(8,128)(2,1)} collective-permute-done((bf16[520,1280]{1,0:T(8,128)(2,1)S(1)}, bf16[520,1280]{1,0:T(8,128)(2,1)}, u32[]{:S(2)}, u32[]{:S(2)}) %collective-permute-start.9) | collective-permute-done | bytes 1331232 | tf_op jit(solution)/shard_map/ppermute | solution.py:203
  36.0 1.7 %collective-permute-start.10 = (bf16[520,1280]{1,0:T(8,128)(2,1)}, bf16[520,1280]{1,0:T(8,128)(2,1)}, u32[]{:S(2)}, u32[]{:S(2)}) collective-permute-start(bf16[520,1280]{1,0:T(8,128)(2,1)} %collective-permute-done.9.refs_6_), channel_id=1, source_target_pairs={{2,3},{3,2},{12,13},{13,12},{20,21},{21,20},{26,27},{27,26}} | collective-permute-start | bytes 3993608 | tf_op jit(solution)/shard_map/ppermute | solution.py:203
  37.8 0.0 collective-permute-done.refs_0_
  37.8 1.7 %collective-permute-start.1 = (bf16[520,1280]{1,0:T(8,128)(2,1)}, bf16[520,1280]{1,0:T(8,128)(2,1)}, u32[]{:S(2)}, u32[]{:S(2)}) collective-permute-start(bf16[520,1280]{1,0:T(8,128)(2,1)} %collective-permute-done.refs_0_), channel_id=1, source_target_pairs={{2,3},{3,2},{12,13},{13,12},{20,21},{21,20},{26,27},{27,26}} | collective-permute-start | bytes 3993608 | tf_op jit(solution)/shard_map/ppermute | solution.py:203
  39.5 0.1 pad_add_fusion.where_ref
  39.6 0.0 copy-start.1
  39.6 0.0 collective-permute-done.2.refs_3_
  39.6 0.0 collective-permute-done.8.refs_5_
  39.6 0.0 collective-permute-done.10.refs_7_
  39.6 0.0 collective-permute-done.1.refs_1_
  39.6 13.0 %shard_map.61 = (bf16[128,512]{1,0:T(8,128)(2,1)S(1)}, bf16[128,512]{1,0:T(8,128)(2,1)S(1)}, bf16[128,512]{1,0:T(8,128)(2,1)S(1)}, bf16[128,512]{1,0:T(8,128)(2,...) custom-call(s32[3]{0:T(128)S(1)} %pad_add_fusion.where_ref, ...), custom_call_target="tpu_custom_call" | custom-call | flops 5368709120 | tf_op jit(solution)/shard_map/pallas_call | solution.py:246
  52.5 0.7 collective-permute-start.11
  53.2 0.7 collective-permute-start.12
  53.9 1.3 %collective-permute-start.13 = (bf16[128,512]{1,0:T(8,128)(2,1)S(1)}, bf16[128,512]{1,0:T(8,128)(2,1)S(1)}, u32[]{:S(2)}, u32[]{:S(2)}) collective-permute-start(bf16[128,512]{1,0:T(8,128)(2,1)S(1)} %get-tuple-element.21), channel_id=1, source_target_pairs={{2,6},{3,7},{12,8},{13,9},{20,16},{21,17},{26,30},{27,31}} | collective-permute-start | bytes 393224 | tf_op jit(solution)/shard_map/ppermute | solution.py:203
  55.2 0.7 collective-permute-start.14
  55.9 0.7 collective-permute-start.15
  56.6 0.0 collective-permute-done.11.refs_0_
  56.6 0.7 collective-permute-start.16
  57.2 0.0 collective-permute-done.12.refs_2_
  57.3 1.3 %collective-permute-start.17 = (bf16[128,512]{1,0:T(8,128)(2,1)S(1)}, bf16[128,512]{1,0:T(8,128)(2,1)S(1)}, u32[]{:S(2)}, u32[]{:S(2)}) collective-permute-start(bf16[128,512]{1,0:T(8,128)(2,1)S(1)} %get-tuple-element.25), channel_id=1, source_target_pairs={{2,7},{3,6},{12,9},{13,8},{20,17},{21,16},{26,31},{27,30}} | collective-permute-start | bytes 393224 | tf_op jit(solution)/shard_map/ppermute | solution.py:203
  58.6 23.5 %collective-permute-done.13.refs_3_ = bf16[128,512]{1,0:T(8,128)(2,1)S(1)} collective-permute-done((bf16[128,512]{1,0:T(8,128)(2,1)S(1)}, bf16[128,512]{1,0:T(8,128)(2,1)S(1)}, u32[]{:S(2)}, u32[]{:S(2)}) %collective-permute-start.13) | collective-permute-done | bytes 131104 | tf_op jit(solution)/shard_map/ppermute | solution.py:203
  82.0 0.0 collective-permute-done.14.refs_4_
  82.0 0.0 collective-permute-done.15.refs_5_
  82.0 0.0 collective-permute-done.16.refs_6_
  82.0 6.4 %collective-permute-done.17.refs_7_ = bf16[128,512]{1,0:T(8,128)(2,1)S(1)} collective-permute-done((bf16[128,512]{1,0:T(8,128)(2,1)S(1)}, bf16[128,512]{1,0:T(8,128)(2,1)S(1)}, u32[]{:S(2)}, u32[]{:S(2)}) %collective-permute-start.17) | collective-permute-done | bytes 131104 | tf_op jit(solution)/shard_map/ppermute | solution.py:203
  88.4 0.0 copy-done.1
  88.4 1.4 %shard_map.62 = (f32[128,1024]{1,0:T(8,128)}, f32[128,128]{1,0:T(8,128)}) custom-call(s32[3]{0:T(128)S(1)} %pad_add_fusion.where_ref, bf16[1024,128]{1,0:T(8,128)(2,1)S(1)} %copy-done.1, bf16[128,512]{1,0:T(8,128)(2,1)S(1)} %collective-permute-done.11.refs_0_, bf16[128,512]{1,0:T(8,128)(2,1)S(1)} %get-tuple-element.19.refs_1_, ...), custom_call_target="tpu_custom_call" | custom-call | tf_op jit(solution)/shard_map/pallas_call | solution.py:266
Async XLA Ops:
  0.6 1.2 %copy-start = (bf16[512,1024]{1,0:T(8,128)(2,1)S(1)}, bf16[512,1024]{1,0:T(8,128)(2,1)}, u32[]{:S(2)}) copy-start(bf16[512,1024]{1,0:T(8,128)(2,1)} %p_ref.1) | copy-start | bytes 3145732
  1.9 0.9 %copy-start.2 = (bf16[8,128,128]{2,1,0:T(8,128)(2,1)S(1)}, bf16[8,128,128]{2,1,0:T(8,128)(2,1)}, u32[]{:S(2)}) copy-start(bf16[8,128,128]{2,1,0:T(8,128)(2,1)} %t_ref.1) | copy-start | bytes 786436
  2.8 0.7 copy-start.3
  3.9 32.1 %collective-permute-start.9 = (bf16[520,1280]{1,0:T(8,128)(2,1)S(1)}, bf16[520,1280]{1,0:T(8,128)(2,1)}, u32[]{:S(2)}, u32[]{:S(2)}) collective-permute-start(bf16[520,1280]{1,0:T(8,128)(2,1)S(1)} %get-tuple-element.14.refs_2_), channel_id=1, source_target_pairs={{6,2},{7,3},{8,12},{9,13},{16,20},{17,21},{30,26},{31,27}} | collective-permute-start | bytes 3993608 | tf_op jit(solution)/shard_map/ppermute | solution.py:203
  9.2 28.6 %collective-permute-start = (bf16[520,1280]{1,0:T(8,128)(2,1)S(1)}, bf16[520,1280]{1,0:T(8,128)(2,1)}, u32[]{:S(2)}, u32[]{:S(2)}) collective-permute-start(bf16[520,1280]{1,0:T(8,128)(2,1)S(1)} %get-tuple-element.14.refs_2_), channel_id=1, source_target_pairs={{0,2},{1,3},{14,12},{15,13},{22,20},{23,21},{24,26},{25,27}} | collective-permute-start | bytes 3993608 | tf_op jit(solution)/shard_map/ppermute | solution.py:203
  10.9 1.4 %collective-permute-start.4 = (bf16[200,1280]{1,0:T(8,128)(2,1)S(1)}, bf16[200,1280]{1,0:T(8,128)(2,1)S(1)}, u32[]{:S(2)}, u32[]{:S(2)}) collective-permute-start(bf16[200,1280]{1,0:T(8,128)(2,1)S(1)} %get-tuple-element.16), channel_id=1, source_target_pairs={{4,12},{5,13},{10,2},{11,3},{18,26},{19,27},{28,20},{29,21}} | collective-permute-start | bytes 1536008 | tf_op jit(solution)/shard_map/ppermute | solution.py:203
  11.6 1.4 %collective-permute-start.6 = (bf16[192,1280]{1,0:T(8,128)(2,1)S(1)}, bf16[192,1280]{1,0:T(8,128)(2,1)S(1)}, u32[]{:S(2)}, u32[]{:S(2)}) collective-permute-start(bf16[192,1280]{1,0:T(8,128)(2,1)S(1)} %get-tuple-element.17), channel_id=1, source_target_pairs={{4,20},{5,21},{10,26},{11,27},{18,2},{19,3},{28,12},{29,13}} | collective-permute-start | bytes 1474568 | tf_op jit(solution)/shard_map/ppermute | solution.py:203
  12.3 3.9 %collective-permute-start.5 = (bf16[200,1280]{1,0:T(8,128)(2,1)S(1)}, bf16[200,1280]{1,0:T(8,128)(2,1)S(1)}, u32[]{:S(2)}, u32[]{:S(2)}) collective-permute-start(bf16[200,1280]{1,0:T(8,128)(2,1)S(1)} %collective-permute-done.4), channel_id=1, source_target_pairs={{12,2},{13,3},{2,12},{3,13},{26,20},{27,21},{20,26},{21,27}} | collective-permute-start | bytes 1536008 | tf_op jit(solution)/shard_map/ppermute | solution.py:203
  13.0 3.2 %collective-permute-start.7 = (bf16[192,1280]{1,0:T(8,128)(2,1)S(1)}, bf16[192,1280]{1,0:T(8,128)(2,1)S(1)}, u32[]{:S(2)}, u32[]{:S(2)}) collective-permute-start(bf16[192,1280]{1,0:T(8,128)(2,1)S(1)} %collective-permute-done.6), channel_id=1, source_target_pairs={{20,2},{21,3},{26,12},{27,13},{2,20},{3,21},{12,26},{13,27}} | collective-permute-start | bytes 1474568 | tf_op jit(solution)/shard_map/ppermute | solution.py:203
  13.7 0.7 collective-permute-start.3
  14.4 25.2 %collective-permute-start.2 = (bf16[520,1280]{1,0:T(8,128)(2,1)S(1)}, bf16[520,1280]{1,0:T(8,128)(2,1)}, u32[]{:S(2)}, u32[]{:S(2)}) collective-permute-start(bf16[520,1280]{1,0:T(8,128)(2,1)S(1)} %get-tuple-element.14.refs_2_), channel_id=1, source_target_pairs={{2,3},{3,2},{12,13},{13,12},{20,21},{21,20},{26,27},{27,26}} | collective-permute-start | bytes 3993608 | tf_op jit(solution)/shard_map/ppermute | solution.py:203
  16.2 23.3 %collective-permute-start.8 = (bf16[520,1280]{1,0:T(8,128)(2,1)S(1)}, bf16[520,1280]{1,0:T(8,128)(2,1)}, u32[]{:S(2)}, u32[]{:S(2)}) collective-permute-start(bf16[520,1280]{1,0:T(8,128)(2,1)S(1)} %shard_map.60.refs_4_), channel_id=1, source_target_pairs={{2,3},{3,2},{12,13},{13,12},{20,21},{21,20},{26,27},{27,26}} | collective-permute-start | bytes 3993608 | tf_op jit(solution)/shard_map/ppermute | solution.py:203
  36.0 3.5 %collective-permute-start.10 = (bf16[520,1280]{1,0:T(8,128)(2,1)}, bf16[520,1280]{1,0:T(8,128)(2,1)}, u32[]{:S(2)}, u32[]{:S(2)}) collective-permute-start(bf16[520,1280]{1,0:T(8,128)(2,1)} %collective-permute-done.9.refs_6_), channel_id=1, source_target_pairs={{2,3},{3,2},{12,13},{13,12},{20,21},{21,20},{26,27},{27,26}} | collective-permute-start | bytes 3993608 | tf_op jit(solution)/shard_map/ppermute | solution.py:203
  37.8 1.8 %collective-permute-start.1 = (bf16[520,1280]{1,0:T(8,128)(2,1)}, bf16[520,1280]{1,0:T(8,128)(2,1)}, u32[]{:S(2)}, u32[]{:S(2)}) collective-permute-start(bf16[520,1280]{1,0:T(8,128)(2,1)} %collective-permute-done.refs_0_), channel_id=1, source_target_pairs={{2,3},{3,2},{12,13},{13,12},{20,21},{21,20},{26,27},{27,26}} | collective-permute-start | bytes 3993608 | tf_op jit(solution)/shard_map/ppermute | solution.py:203
  39.6 48.9 %copy-start.1 = (bf16[1024,128]{1,0:T(8,128)(2,1)S(1)}, bf16[1024,128]{1,0:T(8,128)(2,1)}, u32[]{:S(2)}) copy-start(bf16[1024,128]{1,0:T(8,128)(2,1)} %trial_ref.1) | copy-start | bytes 786436
  52.5 4.0 %collective-permute-start.11 = (bf16[128,512]{1,0:T(8,128)(2,1)S(1)}, bf16[128,512]{1,0:T(8,128)(2,1)S(1)}, u32[]{:S(2)}, u32[]{:S(2)}) collective-permute-start(bf16[128,512]{1,0:T(8,128)(2,1)S(1)} %get-tuple-element.18), channel_id=1, source_target_pairs={{2,0},{3,1},{12,14},{13,15},{20,22},{21,23},{26,24},{27,25}} | collective-permute-start | bytes 393224 | tf_op jit(solution)/shard_map/ppermute | solution.py:203
  53.2 4.0 %collective-permute-start.12 = (bf16[128,512]{1,0:T(8,128)(2,1)S(1)}, bf16[128,512]{1,0:T(8,128)(2,1)S(1)}, u32[]{:S(2)}, u32[]{:S(2)}) collective-permute-start(bf16[128,512]{1,0:T(8,128)(2,1)S(1)} %get-tuple-element.20), channel_id=1, source_target_pairs={{2,4},{3,5},{12,10},{13,11},{20,18},{21,19},{26,28},{27,29}} | collective-permute-start | bytes 393224 | tf_op jit(solution)/shard_map/ppermute | solution.py:203
  53.9 28.1 %collective-permute-start.13 = (bf16[128,512]{1,0:T(8,128)(2,1)S(1)}, bf16[128,512]{1,0:T(8,128)(2,1)S(1)}, u32[]{:S(2)}, u32[]{:S(2)}) collective-permute-start(bf16[128,512]{1,0:T(8,128)(2,1)S(1)} %get-tuple-element.21), channel_id=1, source_target_pairs={{2,6},{3,7},{12,8},{13,9},{20,16},{21,17},{26,30},{27,31}} | collective-permute-start | bytes 393224 | tf_op jit(solution)/shard_map/ppermute | solution.py:203
  55.2 26.8 %collective-permute-start.14 = (bf16[128,512]{1,0:T(8,128)(2,1)S(1)}, bf16[128,512]{1,0:T(8,128)(2,1)S(1)}, u32[]{:S(2)}, u32[]{:S(2)}) collective-permute-start(bf16[128,512]{1,0:T(8,128)(2,1)S(1)} %get-tuple-element.22), channel_id=1, source_target_pairs={{2,1},{3,0},{12,15},{13,14},{20,23},{21,22},{26,25},{27,24}} | collective-permute-start | bytes 393224 | tf_op jit(solution)/shard_map/ppermute | solution.py:203
  55.9 26.1 %collective-permute-start.15 = (bf16[128,512]{1,0:T(8,128)(2,1)S(1)}, bf16[128,512]{1,0:T(8,128)(2,1)S(1)}, u32[]{:S(2)}, u32[]{:S(2)}) collective-permute-start(bf16[128,512]{1,0:T(8,128)(2,1)S(1)} %get-tuple-element.23), channel_id=1, source_target_pairs={{2,3},{3,2},{12,13},{13,12},{20,21},{21,20},{26,27},{27,26}} | collective-permute-start | bytes 393224 | tf_op jit(solution)/shard_map/ppermute | solution.py:203
  56.6 25.5 %collective-permute-start.16 = (bf16[128,512]{1,0:T(8,128)(2,1)S(1)}, bf16[128,512]{1,0:T(8,128)(2,1)S(1)}, u32[]{:S(2)}, u32[]{:S(2)}) collective-permute-start(bf16[128,512]{1,0:T(8,128)(2,1)S(1)} %get-tuple-element.24), channel_id=1, source_target_pairs={{2,5},{3,4},{12,11},{13,10},{20,19},{21,18},{26,29},{27,28}} | collective-permute-start | bytes 393224 | tf_op jit(solution)/shard_map/ppermute | solution.py:203
  57.3 31.2 %collective-permute-start.17 = (bf16[128,512]{1,0:T(8,128)(2,1)S(1)}, bf16[128,512]{1,0:T(8,128)(2,1)S(1)}, u32[]{:S(2)}, u32[]{:S(2)}) collective-permute-start(bf16[128,512]{1,0:T(8,128)(2,1)S(1)} %get-tuple-element.25), channel_id=1, source_target_pairs={{2,7},{3,6},{12,9},{13,8},{20,17},{21,16},{26,31},{27,30}} | collective-permute-start | bytes 393224 | tf_op jit(solution)/shard_map/ppermute | solution.py:203
